TPU v7x, 16 devices: a 4x2x1 block of a 4x4x8 slice. The times are simulated.
16 devices in a mesh: dp: 2 (over y, z), tp: 8 (over x, core).
Axes of the slice: x: 4, y: 2, z: 1, core: 2. Of those that a mesh axis runs over, the one named last changes fastest.
The devices are a block of a 4x4x8 slice.
Arguments:
- hidden: bfloat16 [2, 256, 9216], P('dp'), parts along dimension 0
- ln_gain: float32 [9216], replicated
- ln_bias: float32 [9216], replicated
- embedding: bfloat16 [51200, 9216], P('tp')
- targets: int32 [2, 256], P('dp'), parts along dimension 0
- score_mask: int32 [2, 256], P('dp'), parts along dimension 0
Outputs:
- output 1: float32 [2, 256], P('dp'), parts along dimension 0
- output 2: float32 [2, 256], P('dp'), parts along dimension 0
- output 3: float32 [2], P('dp'), parts along dimension 0
- output 4: float32 [2, 256], P('dp'), parts along dimension 0
There are 2 independent parts. A program takes and returns all parts, laid end to end along the dimension named above; an argument that names none is the same for every part.
All inputs are finite; a program needn't handle non-finite values.
Results may differ from a plain program's by a relative error of at most 0.001.
Values sent between devices are 32-bit elements.
A program may use at most 768 MiB of HBM per device.

v0:
```python
import jax
import jax.numpy as jnp
from jax import lax
from jax.sharding import PartitionSpec as P

OPT_VOCAB = 50272
LN_EPS = 1e-5


def layer_norm(hidden, ln_gain, ln_bias):
    hidden_f = hidden.astype(jnp.float32)
    row_mean = jnp.mean(hidden_f, axis=-1, keepdims=True)
    centered = hidden_f - row_mean
    row_var = jnp.mean(centered * centered, axis=-1, keepdims=True)
    return (centered * lax.rsqrt(row_var + LN_EPS) * ln_gain + ln_bias).astype(jnp.bfloat16)


def solution(mesh):
    def local_part(hidden, ln_gain, ln_bias, embedding, targets, score_mask):
        shard_rows = embedding.shape[0]
        vocab_ids = lax.axis_index("tp") * shard_rows + jnp.arange(shard_rows)
        normed = layer_norm(hidden, ln_gain, ln_bias)
        logits = jnp.einsum("bsd,vd->bsv", normed, embedding, preferred_element_type=jnp.float32)
        logits = jnp.where(vocab_ids < OPT_VOCAB, logits, -jnp.inf)
        row_max = lax.pmax(jnp.max(logits, axis=-1), "tp")
        exp_sum = jnp.sum(jnp.exp(logits - row_max[..., None]), axis=-1)
        target_part = jnp.sum(jnp.where(vocab_ids == targets[..., None], logits, 0.0), axis=-1)
        combined = lax.psum(jnp.stack([exp_sum, target_part]), "tp")
        log_norm = row_max + jnp.log(combined[0])
        token_logp = (combined[1] - log_norm) * score_mask.astype(jnp.float32)
        return log_norm, token_logp, jnp.sum(token_logp, axis=-1), row_max - log_norm

    row_spec = P("dp", None)
    return jax.shard_map(local_part, mesh=mesh, in_specs=(P("dp", None, None), P(), P(), P("tp", None), row_spec, row_spec), out_specs=(row_spec, row_spec, P("dp"), row_spec), check_vma=False)
```

profile of v0, /device:TPU:113, one launch (start us, length us, event | category | flops | bytes accessed | tf_op | source)
XLA Modules:
  0.0 87.1 jit_solution(18395698196504247013)
XLA Ops:
  0.6 0.0 copy-start
  0.6 0.0 copy-start.4
  0.7 0.0 copy-start.5
  0.7 3.2 %convert_reduce_fusion = f32[256]{0:T(256)S(1)} fusion(bf16[1,256,9216]{2,1,0:T(8,128)(2,1)} %param.6), kind=kLoop, calls=%fused_computation.1 | loop fusion | flops 4718336 | bytes 4719616 | tf_op jit(solution)/shard_map/reduce_sum | solution.py:12
  3.9 0.5 copy-done
  4.4 1.4 %fusion.2 = f32[256]{0:T(256)S(1)} fusion(bf16[1,256,9216]{2,1,0:T(8,128)(2,1)S(1)} %copy-done, f32[256]{0:T(256)S(1)} %broadcast_multiply_fusion), kind=kLoop, calls=%fused_computation.4 | loop fusion | flops 9436928 | bytes 4720640 | tf_op jit(solution)/shard_map/reduce_sum | solution.py:14
  5.8 0.0 copy-done.4
  5.8 0.0 copy-done.5
  5.8 0.0 copy-start.2
  5.8 47.2 %fusion.20 = (f32[256]{0:T(256)S(1)}, f32[256,6400]{1,0:T(8,128)}) fusion(bf16[6400,9216]{1,0:T(8,128)(2,1)} %param.9, bf16[1,256,9216]{2,1,0:T(8,128)(2,1)} %param.6, f32[9216]{0:T(1024)S(1)} %copy-done.4, f32[9216]{0:T(1024)S(1)} %copy-done.5, f32[256]{0:T(256)S(1)} %add_rsqrt_fusion, f32[256]{0:T(256)S(1)} %broadcast_multiply_fusion, ...), kind=kOutput, calls=%fused_computation.29 | convolution fusion | flops 30216421376 | bytes 129320192 | tf_op jit(solution)/shard_map/bsd,vd->bsv/dot_general | solution.py:23
  53.0 0.0 copy-start.3
  53.0 13.5 %pmax.7 = f32[1,256]{1,0:T(1,128)S(1)} all-reduce(f32[1,256]{1,0:T(1,128)S(1)} %bitcast.31), channel_id=1, replica_groups=mesh['dp'=2,'tp'=8] {'tp'}, use_global_device_ids=true, to_apply=%region_3.4 | all-reduce | flops 256 | bytes 2048 | tf_op jit(solution)/shard_map/pmax | solution.py:25
  66.6 0.0 copy-done.2
  66.6 3.9 %exponential_reduce_fusion = (f32[256]{0:T(256)S(1)}, f32[256]{0:T(256)S(1)}) fusion(f32[256,6400]{1,0:T(8,128)} %get-tuple-element.11, f32[256]{0:T(256)S(1)} %bitcast.27, s32[256]{0:T(256)S(1)} %bitcast.30, s32[6400]{0:T(1024)S(1)} %iota_add_fusion), kind=kLoop, calls=%fused_computation.10 | loop fusion | flops 8191488 | bytes 6583296 | tf_op jit(solution)/shard_map/reduce_sum | solution.py:26
  70.5 14.8 %psum.7 = f32[2,1,256]{2,1,0:T(1,128)S(1)} all-reduce(f32[2,1,256]{2,1,0:T(1,128)S(1)} %pad_maximum_fusion), channel_id=1, replica_groups=mesh['dp'=2,'tp'=8] {'tp'}, use_global_device_ids=true, to_apply=%region_6.7 | all-reduce | flops 512 | bytes 4096 | tf_op jit(solution)/shard_map/psum | solution.py:28
  85.3 0.6 fusion.16
  85.9 0.0 copy-start.1
  85.9 0.0 copy-done.3
  85.9 1.2 %fusion.18 = (f32[]{:T(128)}, f32[1,256]{1,0:T(1,128)}) fusion(s32[1,256]{1,0:T(1,128)S(1)} %copy-done.3, f32[1,256]{1,0:T(1,128)S(1)} %get-tuple-element.7, f32[2,1,256]{2,1,0:T(1,128)S(1)} %psum.7), kind=kLoop, calls=%fused_computation.28 | loop fusion | flops 1023 | bytes 4100 | tf_op jit(solution)/shard_map/reduce_sum | solution.py:31
  87.0 0.0 copy-done.1
  (5 shorter events, 0.0 us)
Async XLA Ops:
  0.6 3.8 %copy-start = (bf16[1,256,9216]{2,1,0:T(8,128)(2,1)S(1)}, bf16[1,256,9216]{2,1,0:T(8,128)(2,1)}, u32[]{:S(2)}) copy-start(bf16[1,256,9216]{2,1,0:T(8,128)(2,1)} %param.6) | copy-start | bytes 14155780
  0.6 5.1 %copy-start.4 = (f32[9216]{0:T(1024)S(1)}, f32[9216]{0:T(1024)}, u32[]{:S(2)}) copy-start(f32[9216]{0:T(1024)} %param.8) | copy-start | bytes 110596
  0.7 5.1 %copy-start.5 = (f32[9216]{0:T(1024)S(1)}, f32[9216]{0:T(1024)}, u32[]{:S(2)}) copy-start(f32[9216]{0:T(1024)} %param.7) | copy-start | bytes 110596
  5.8 60.8 %copy-start.2 = (s32[1,256]{1,0:T(1,128)S(1)}, s32[1,256]{1,0:T(1,128)}, u32[]{:S(2)}) copy-start(s32[1,256]{1,0:T(1,128)} %param.10) | copy-start | bytes 3076
  53.0 32.9 %copy-start.3 = (s32[1,256]{1,0:T(1,128)S(1)}, s32[1,256]{1,0:T(1,128)}, u32[]{:S(2)}) copy-start(s32[1,256]{1,0:T(1,128)} %param.11) | copy-start | bytes 3076
  85.9 1.2 %copy-start.1 = (f32[1,256]{1,0:T(1,128)}, f32[1,256]{1,0:T(1,128)S(1)}, u32[]{:S(2)}) copy-start(f32[1,256]{1,0:T(1,128)S(1)} %get-tuple-element.7) | copy-start | bytes 3076
where the time goes:
time: 87.3 us; the launch traced here: 87.1 us
  matrix products  47.2 us (54%)
  blocking collectives  28.4 us (33%)
  other arithmetic  10.3 us (12%)
    dot_general x1, matrix products, local_part(): jnp.einsum('bsd,vd->bsv', normed, embedding, preferred_element_type=jnp.f...  47.2 us
    psum x1, blocking collectives, local_part(): combined = lax.psum(jnp.stack([exp_sum, target_part]), 'tp')  14.8 us
    pmax x1, blocking collectives, local_part(): row_max = lax.pmax(jnp.max(logits, axis=-1), 'tp')  13.5 us
    reduce_sum x1, other arithmetic, local_part(): exp_sum = jnp.sum(jnp.exp(logits - row_max[..., None]), axis=-1)  3.9 us
    reduce_sum x1, other arithmetic, layer_norm(): row_mean = jnp.mean(hidden_f, axis=-1, keepdims=True)  3.21 us

commit v1 on v0

v1 whole, which is shorter than its diff:
```python
import functools

import jax
import jax.numpy as jnp
from jax import lax
from jax.experimental import pallas as pl
from jax.experimental.pallas import tpu as pltpu
from jax.sharding import PartitionSpec as P

OPT_VOCAB = 50272
LN_EPS = 1e-5

TILE = 256
BLOCK = 256
PIECE = 64
LANES = 128
RING = 12
PARTS = 3
HID_PARTS = 4
F32 = jnp.float32


def head_kernel(hid_hbm, gain_hbm, bias_hbm, emb_hbm, tgt_hbm, stats_ref,
                h, ring, z, gain, bias, tgt, mean_b, rstd_b, part, m8, s8, t8, small_sem, hid_sem, ring_sem):
    tokens, width = h.shape
    rows = emb_hbm.shape[0]
    n_blocks = rows // BLOCK
    passes = width // (2 * TILE)
    part_width = width // PARTS
    part_passes = passes // PARTS
    hid_rows = tokens // HID_PARTS
    me = lax.axis_index("tp")
    base = me * rows

    def hid_copy(i):
        at = pl.ds(i * hid_rows, hid_rows)
        return pltpu.make_async_copy(hid_hbm.at[0, at], h.at[at], hid_sem.at[i])

    def ring_copy(b, i):
        slot = lax.rem(b, RING)
        cols = pl.ds(i * part_width, part_width)
        return pltpu.make_async_copy(
            emb_hbm.at[pl.ds(b * BLOCK, BLOCK), cols], ring.at[slot, :, cols], ring_sem.at[slot, i])

    small = [pltpu.make_async_copy(src, dst, small_sem.at[i]) for i, (src, dst) in enumerate(
        ((gain_hbm, gain), (bias_hbm, bias), (tgt_hbm, tgt)))]

    for i in range(HID_PARTS):
        hid_copy(i).start()
    for copy in small:
        copy.start()
    for b in range(min(RING, n_blocks)):
        for i in range(PARTS):
            ring_copy(b, i).start()

    def lane_sum(r, n, fn):
        acc = [jnp.zeros((n, LANES), F32) for _ in range(2)]
        for c in range(width // LANES):
            acc[c % 2] += fn(h[pl.ds(r, n), pl.ds(c * LANES, LANES)].astype(F32))
        return acc[0] + acc[1]

    group = 16

    def mean_rows(i):
        for g in range(hid_rows // group):
            r = i * hid_rows + g * group
            part[pl.ds(r, group)] = lane_sum(r, group, lambda x: x)
        at = pl.ds(i * hid_rows, hid_rows)
        mean = jnp.sum(part[at], axis=-1, keepdims=True) * (1.0 / width)
        mean_b[at] = jnp.broadcast_to(mean, (hid_rows, LANES))

    def var_rows(i):
        for g in range(hid_rows // group):
            r = i * hid_rows + g * group
            mean = mean_b[pl.ds(r, group)]
            part[pl.ds(r, group)] = lane_sum(r, group, lambda x: (x - mean) * (x - mean))
        at = pl.ds(i * hid_rows, hid_rows)
        var = jnp.sum(part[at], axis=-1, keepdims=True) * (1.0 / width)
        rstd_b[at] = jnp.broadcast_to(lax.rsqrt(var + LN_EPS), (hid_rows, LANES))

    for i in range(HID_PARTS):
        hid_copy(i).wait()
        mean_rows(i)
        if i:
            var_rows(i - 1)
    var_rows(HID_PARTS - 1)

    for copy in small:
        copy.wait()
    m8[...] = jnp.full_like(m8, jnp.finfo(F32).min)
    s8[...] = jnp.zeros_like(s8)
    t8[...] = jnp.zeros_like(t8)

    def normalize(k):
        for c in range(TILE // LANES):
            cols = pl.ds(k * TILE + c * LANES, LANES)
            x = h[:, cols].astype(F32)
            x = (x - mean_b[...]) * rstd_b[...] * gain[:, cols] + bias[:, cols]
            h[:, cols] = x.astype(h.dtype)

    def matmuls(*accs):
        n_piece = BLOCK // PIECE
        accs = [[list(accs[(w * 2 + q) * n_piece:(w * 2 + q + 1) * n_piece]) for q in range(2)] for w in range(2)]

        for which in accs:
            for q in which:
                for acc in q:
                    z[pl.ds(0, PIECE)] = pltpu.matmul_pop(acc)

        def push(j, q):
            k = 2 * j + q
            pltpu.matmul_push_rhs(h[:, pl.ds(k * TILE, TILE)], staging_register=j % 2, mxu_index=q, transpose=True)

        def accumulate(b, j, q, which):
            slot = lax.rem(b, RING)
            cols = pl.ds((2 * j + q) * TILE, TILE)
            for p in range(n_piece):
                lhs = ring[slot, pl.ds(p * PIECE, PIECE), cols]
                pltpu.matmul_acc_lhs(accs[which][q][p], lhs, load_staged_rhs=j % 2 if p == 0 else None)

        def drain(b, which, first, last):
            offset = base + b * BLOCK
            target = tgt[...] - offset
            limit = OPT_VOCAB - offset
            top, picked = m8[1], t8[...]
            for p in range(first, last):
                logits = pltpu.matmul_pop(accs[which][0][p]) + pltpu.matmul_pop(accs[which][1][p])
                row = lax.broadcasted_iota(jnp.int32, logits.shape, 0) + p * PIECE
                logits = jnp.where(row < limit, logits, -jnp.inf)
                z[pl.ds(p * PIECE, PIECE)] = logits
                top = jnp.maximum(top, jnp.max(logits.reshape(PIECE // 8, 8, tokens), axis=0))
                hit = jnp.where(row == target, logits, 0.0)
                picked = picked + jnp.sum(hit.reshape(PIECE // 8, 8, tokens), axis=0)
            m8[1] = top
            t8[...] = picked

        def exps(first, last):
            top = m8[1]
            total = s8[...]
            if first == 0:
                total = total * jnp.exp(m8[0] - top)
                m8[0] = top
            for p in range(first, last):
                e = jnp.exp(z[pl.ds(p * PIECE, PIECE)].reshape(PIECE // 8, 8, tokens) - top[None])
                total = total + jnp.sum(e, axis=0)
            s8[...] = total

        def block(b, which, refill=None, drained=None, norm=False, last=False):
            for j in range(passes):
                if j % part_passes == 0:
                    ring_copy(b, j // part_passes).wait()
                    if j == 0 and refill is not None:
                        refill()
                for q in range(2):
                    if norm and j + 1 < passes:
                        normalize(2 * (j + 1) + q)
                    if not (last and j + 1 == passes):
                        push((j + 1) % passes, q)
                for q in range(2):
                    accumulate(b, j, q, which)
                if drained is not None:
                    if j in (2, 3):
                        half = n_piece // 2
                        drain(*drained, (j - 2) * half, (j - 1) * half)
                    if j in (4, 5):
                        exps((j - 4) * half, (j - 3) * half)

        def refill(b):
            def start():
                @pl.when(b - 1 + RING < n_blocks)
                def _():
                    for i in range(PARTS):
                        ring_copy(b - 1 + RING, i).start()
            return start

        for q in range(2):
            normalize(q)
            push(0, q)
        block(0, 0, norm=True)

        def two(i, carry):
            b = 2 * i + 1
            block(b, 1, refill(b), drained=(b - 1, 0))
            block(b + 1, 0, refill(b + 1), drained=(b, 1))
            return carry

        lax.fori_loop(0, (n_blocks - 3) // 2, two, 0)
        b = n_blocks - 2
        block(b, 1, drained=(b - 1, 0))
        block(b + 1, 0, drained=(b, 1), last=True)
        drain(b + 1, 0, 0, n_piece)
        exps(0, n_piece)

    pl.run_scoped(matmuls, *[pltpu.ACC(q)((PIECE, TILE), F32)
                             for _ in range(2) for q in range(2) for _ in range(BLOCK // PIECE)])

    top = jnp.max(m8[0], axis=0, keepdims=True)
    total = jnp.sum(s8[...] * jnp.exp(m8[0] - top), axis=0, keepdims=True)
    picked = jnp.sum(t8[...], axis=0, keepdims=True)
    stats_ref[...] = jnp.concatenate([top, total, picked], axis=1)


def combine_kernel(n_tp, stats_ref, mask, norm_ref, logp_ref, seq_ref, top_ref, box, send_sem, recv_sem):
    tokens = mask.shape[1]
    me = lax.axis_index("tp")

    def peer(d):
        return lax.rem(me + d, n_tp)

    def exchange(d, slot):
        return pltpu.make_async_remote_copy(
            src_ref=stats_ref, dst_ref=box.at[slot], send_sem=send_sem.at[d], recv_sem=recv_sem.at[slot],
            device_id={"tp": peer(d)}, device_id_type=pl.DeviceIdType.MESH)

    barrier = pltpu.get_barrier_semaphore()
    for d in range(1, n_tp):
        pl.semaphore_signal(barrier, inc=1, device_id={"tp": peer(d)}, device_id_type=pl.DeviceIdType.MESH)
    pl.semaphore_wait(barrier, n_tp - 1)
    for d in range(1, n_tp):
        exchange(d, me).start()
    box[me] = stats_ref[...]
    for d in range(1, n_tp):
        exchange(d, peer(d)).wait_recv()

    boxes = [box[i] for i in range(n_tp)]
    top = functools.reduce(jnp.maximum, [x[:, :tokens] for x in boxes])
    total = sum(x[:, tokens:2 * tokens] * jnp.exp(x[:, :tokens] - top) for x in boxes)
    picked = sum(x[:, 2 * tokens:] for x in boxes)
    log_norm = top + jnp.log(total)
    token_logp = (picked - log_norm) * mask[...].astype(F32)
    norm_ref[...] = log_norm
    logp_ref[...] = token_logp
    top_ref[...] = top - log_norm
    seq_ref[...] = jnp.broadcast_to(jnp.sum(token_logp, axis=-1, keepdims=True), seq_ref.shape)
    for d in range(1, n_tp):
        exchange(d, me).wait_send()


def solution(mesh):
    n_tp = mesh.shape["tp"]

    def local_part(hidden, ln_gain, ln_bias, embedding, targets, score_mask):
        prompts, tokens, width = hidden.shape
        rows = embedding.shape[0]
        assert prompts == 1 and tokens == TILE and rows % (2 * BLOCK) == BLOCK and width % (2 * TILE * PARTS) == 0
        row = jax.ShapeDtypeStruct((prompts, tokens), F32)
        stats = pl.pallas_call(
            head_kernel,
            out_shape=jax.ShapeDtypeStruct((1, 3 * tokens), F32),
            in_specs=[pl.BlockSpec(memory_space=pl.ANY)] * 5,
            out_specs=pl.BlockSpec(memory_space=pltpu.VMEM),
            scratch_shapes=[
                pltpu.VMEM((tokens, width), hidden.dtype),
                pltpu.VMEM((RING, BLOCK, width), embedding.dtype),
                pltpu.VMEM((BLOCK, tokens), F32),
                pltpu.VMEM((1, width), F32),
                pltpu.VMEM((1, width), F32),
                pltpu.VMEM((1, tokens), jnp.int32),
                pltpu.VMEM((tokens, LANES), F32),
                pltpu.VMEM((tokens, LANES), F32),
                pltpu.VMEM((tokens, LANES), F32),
                pltpu.VMEM((2, 8, tokens), F32),
                pltpu.VMEM((8, tokens), F32),
                pltpu.VMEM((8, tokens), F32),
                pltpu.SemaphoreType.DMA((3,)),
                pltpu.SemaphoreType.DMA((HID_PARTS,)),
                pltpu.SemaphoreType.DMA((RING, PARTS)),
            ],
            compiler_params=pltpu.CompilerParams(vmem_limit_bytes=67043328),
            name="head",
        )(hidden, ln_gain.reshape(1, width), ln_bias.reshape(1, width), embedding, targets)
        vmem = pl.BlockSpec(memory_space=pltpu.VMEM)
        log_norm, token_logp, seq, top_logp = pl.pallas_call(
            functools.partial(combine_kernel, n_tp),
            out_shape=(row, row, jax.ShapeDtypeStruct((prompts, LANES), F32), row),
            in_specs=[vmem] * 2,
            out_specs=[vmem] * 4,
            scratch_shapes=[
                pltpu.VMEM((n_tp, 1, 3 * tokens), F32),
                pltpu.SemaphoreType.DMA((n_tp,)),
                pltpu.SemaphoreType.DMA((n_tp,)),
            ],
            compiler_params=pltpu.CompilerParams(collective_id=0, has_side_effects=True),
            name="combine",
        )(stats, score_mask)
        return log_norm, token_logp, seq[:, 0], top_logp

    row_spec = P("dp", None)
    return jax.shard_map(local_part, mesh=mesh,
                         in_specs=(P("dp", None, None), P(), P(), P("tp", None), row_spec, row_spec),
                         out_specs=(row_spec, row_spec, P("dp"), row_spec), check_vma=False)
```

time: 87.3 us -> 71.6 us (0.82)
  Pallas kernels: 0 us -> 65.4 us
  matrix products: 47.2 us -> 0 us
  blocking collectives: 28.4 us -> 0 us
  other arithmetic: 10.3 us -> 0 us
  local copies, waits for them, and re-layouts: 0.51 us -> 3.64 us
  between operations: 0.7 us -> 2.4 us
    pallas_call x0 -> x2, Pallas kernels: none -> 65.4 us  [the longest x1 56.5 us: local_part(): pl.pallas_call(head_kernel, out_shape=jax.ShapeDtypeStruct((1, 3 * tokens...]
    dot_general x1 -> x0, matrix products: 47.2 us -> none  [local_part(): jnp.einsum('bsd,vd->bsv', normed, embedding, preferred_element_type=jnp.f...]
    psum x1 -> x0, blocking collectives: 14.8 us -> none  [local_part(): combined = lax.psum(jnp.stack([exp_sum, target_part]), 'tp')]
    pmax x1 -> x0, blocking collectives: 13.5 us -> none  [local_part(): row_max = lax.pmax(jnp.max(logits, axis=-1), 'tp')]
    reduce_sum x4 -> x0, other arithmetic: 9.67 us -> none  [the longest x1 3.9 us: local_part(): exp_sum = jnp.sum(jnp.exp(logits - row_max[..., None]), axis=-1)]
    unnamed x12 -> x3, local copies, waits for them, and re-layouts: 0.51 us -> 3.64 us
where the time goes in v1:
time: 71.6 us; the launch traced here: 71.4 us
  Pallas kernels  65.4 us (91%)
  local copies, waits for them, and re-layouts  3.64 us (5%)
  between operations  2.4 us (3%)
    pallas_call x1, Pallas kernels, local_part(): pl.pallas_call(head_kernel, out_shape=jax.ShapeDtypeStruct((1, 3 * tokens...  56.5 us
    pallas_call x1, Pallas kernels, local_part(): pl.pallas_call(functools.partial(combine_kernel, n_tp), out_shape=(row, r...  8.84 us
    unnamed x3, local copies, waits for them, and re-layouts  3.64 us

profile of v1, /device:TPU:113, one launch (start us, length us, event | category | flops | bytes accessed | tf_op | source)
XLA Modules:
  0.0 71.4 jit_solution(17737652498579906891)
XLA Ops:
  0.6 56.5 %head.1.stats_ref = f32[1,768]{1,0:T(1,128)} custom-call(bf16[1,256,9216]{2,1,0:T(8,128)(2,1)} %hid_hbm.1, f32[1,9216]{1,0:T(1,128)} %bitcast.4, f32[1,9216]{1,0:T(1,128)} %bitcast.5, bf16[6400,9216]{1,0:T(8,128)(2,1)} %emb_hbm.1, s32[1,256]{1,0:T(1,128)} %tgt_hbm.1), custom_call_target="tpu_custom_call" | custom-call | tf_op jit(solution)/shard_map/head/pallas_call | solution.py:247
  57.2 8.8 %combine.1 = (f32[1,256]{1,0:T(1,128)}, f32[1,256]{1,0:T(1,128)}, f32[1,128]{1,0:T(1,128)}, f32[1,256]{1,0:T(1,128)}) custom-call(f32[1,768]{1,0:T(1,128)} %head.1.stats_ref, s32[1,256]{1,0:T(1,128)} %mask.1), custom_call_target="tpu_custom_call" | custom-call | tf_op jit(solution)/shard_map/combine/pallas_call | solution.py:273
  66.0 1.2 %copy.14 = f32[1,256]{1,0:T(1,128)} copy(f32[1,256]{1,0:T(1,128)} %get-tuple-element.16) | data formatting | bytes 2048
  67.2 1.2 %copy.15 = f32[1,256]{1,0:T(1,128)} copy(f32[1,256]{1,0:T(1,128)} %get-tuple-element.17) | data formatting | bytes 2048
  69.1 1.2 %copy.17 = f32[1,256]{1,0:T(1,128)} copy(f32[1,256]{1,0:T(1,128)} %get-tuple-element.19) | data formatting | bytes 2048

commit v2 on v1

--- a/solution.py
+++ b/solution.py
@@ -18,6 +18,8 @@
 PARTS = 3
 HID_PARTS = 4
 F32 = jnp.float32
+SMALL_VMEM = 1 << 20
+HEAD_VMEM = 61 << 20
 
 
 def head_kernel(hid_hbm, gain_hbm, bias_hbm, emb_hbm, tgt_hbm, stats_ref,
@@ -51,7 +53,7 @@
         copy.start()
     for b in range(min(RING, n_blocks)):
         for i in range(PARTS):
-            ring_copy(b, i).start()
+            ring_copy(b, i).start(priority=1)
 
     def lane_sum(r, n, fn):
         acc = [jnp.zeros((n, LANES), F32) for _ in range(2)]
@@ -170,7 +172,7 @@
                 @pl.when(b - 1 + RING < n_blocks)
                 def _():
                     for i in range(PARTS):
-                        ring_copy(b - 1 + RING, i).start()
+                        ring_copy(b - 1 + RING, i).start(priority=1)
             return start
 
         for q in range(2):
@@ -200,8 +202,7 @@
     stats_ref[...] = jnp.concatenate([top, total, picked], axis=1)
 
 
-def combine_kernel(n_tp, stats_ref, mask, norm_ref, logp_ref, seq_ref, top_ref, box, send_sem, recv_sem):
-    tokens = mask.shape[1]
+def exchange_kernel(n_tp, stats_ref, out_ref, box, send_sem, recv_sem):
     me = lax.axis_index("tp")
 
     def peer(d):
@@ -221,7 +222,14 @@
     box[me] = stats_ref[...]
     for d in range(1, n_tp):
         exchange(d, peer(d)).wait_recv()
-
+    out_ref[...] = box[...]
+    for d in range(1, n_tp):
+        exchange(d, me).wait_send()
+
+
+def finish_kernel(box, mask, norm_ref, logp_ref, seq_ref, top_ref):
+    n_tp, _, width = box.shape
+    tokens = width // 3
     boxes = [box[i] for i in range(n_tp)]
     top = functools.reduce(jnp.maximum, [x[:, :tokens] for x in boxes])
     total = sum(x[:, tokens:2 * tokens] * jnp.exp(x[:, :tokens] - top) for x in boxes)
@@ -232,8 +240,6 @@
     logp_ref[...] = token_logp
     top_ref[...] = top - log_norm
     seq_ref[...] = jnp.broadcast_to(jnp.sum(token_logp, axis=-1, keepdims=True), seq_ref.shape)
-    for d in range(1, n_tp):
-        exchange(d, me).wait_send()
 
 
 def solution(mesh):
@@ -266,23 +272,32 @@
                 pltpu.SemaphoreType.DMA((HID_PARTS,)),
                 pltpu.SemaphoreType.DMA((RING, PARTS)),
             ],
-            compiler_params=pltpu.CompilerParams(vmem_limit_bytes=67043328),
+            compiler_params=pltpu.CompilerParams(vmem_limit_bytes=HEAD_VMEM),
             name="head",
         )(hidden, ln_gain.reshape(1, width), ln_bias.reshape(1, width), embedding, targets)
         vmem = pl.BlockSpec(memory_space=pltpu.VMEM)
-        log_norm, token_logp, seq, top_logp = pl.pallas_call(
-            functools.partial(combine_kernel, n_tp),
-            out_shape=(row, row, jax.ShapeDtypeStruct((prompts, LANES), F32), row),
-            in_specs=[vmem] * 2,
-            out_specs=[vmem] * 4,
+        boxes = pl.pallas_call(
+            functools.partial(exchange_kernel, n_tp),
+            out_shape=jax.ShapeDtypeStruct((n_tp, 1, 3 * tokens), F32),
+            in_specs=[vmem],
+            out_specs=vmem,
             scratch_shapes=[
                 pltpu.VMEM((n_tp, 1, 3 * tokens), F32),
                 pltpu.SemaphoreType.DMA((n_tp,)),
                 pltpu.SemaphoreType.DMA((n_tp,)),
             ],
-            compiler_params=pltpu.CompilerParams(collective_id=0, has_side_effects=True),
-            name="combine",
-        )(stats, score_mask)
+            compiler_params=pltpu.CompilerParams(
+                collective_id=0, has_side_effects=True, vmem_limit_bytes=SMALL_VMEM),
+            name="exchange",
+        )(stats)
+        log_norm, token_logp, seq, top_logp = pl.pallas_call(
+            finish_kernel,
+            out_shape=(row, row, jax.ShapeDtypeStruct((prompts, LANES), F32), row),
+            in_specs=[vmem] * 2,
+            out_specs=[vmem] * 4,
+            compiler_params=pltpu.CompilerParams(vmem_limit_bytes=SMALL_VMEM),
+            name="finish",
+        )(boxes, score_mask)
         return log_norm, token_logp, seq[:, 0], top_logp
 
     row_spec = P("dp", None)

time: 71.6 us -> 50.9 us (0.71)
  Pallas kernels: 65.4 us -> 49.5 us
  local copies, waits for them, and re-layouts: 3.64 us -> 0.67 us
  between operations: 2.4 us -> 0.67 us
    pallas_call x1, Pallas kernels: 56.5 us -> 41.4 us  [local_part(): pl.pallas_call(head_kernel, out_shape=jax.ShapeDtypeStruct((1, 3 * tokens...]
    unnamed x3 -> x4, local copies, waits for them, and re-layouts: 3.64 us -> 0.67 us
    pallas_call x1 -> x2, Pallas kernels: 8.84 us -> 8.11 us  [the longest x1 7.48 us: local_part(): pl.pallas_call(functools.partial(exchange_kernel, n_tp), out_shape=jax.Sh...]
where the time goes in v2:
time: 50.9 us; the launch traced here: 50.8 us
  Pallas kernels  49.5 us (97%)
  local copies, waits for them, and re-layouts  0.67 us (1%)
  between operations  0.67 us (1%)
    pallas_call x1, Pallas kernels, local_part(): pl.pallas_call(head_kernel, out_shape=jax.ShapeDtypeStruct((1, 3 * tokens...  41.4 us
    pallas_call x1, Pallas kernels, local_part(): pl.pallas_call(functools.partial(exchange_kernel, n_tp), out_shape=jax.Sh...  7.48 us

profile of v2, /device:TPU:113, one launch (start us, length us, event | category | flops | bytes accessed | tf_op | source)
XLA Modules:
  0.0 50.8 jit_solution(5936646310873331647)
XLA Ops:
  0.6 0.0 copy-start.1
  0.6 41.4 %head.1.stats_ref = f32[1,768]{1,0:T(1,128)} custom-call(bf16[1,256,9216]{2,1,0:T(8,128)(2,1)} %hid_hbm.1, f32[1,9216]{1,0:T(1,128)} %bitcast.4, f32[1,9216]{1,0:T(1,128)} %bitcast.5, bf16[6400,9216]{1,0:T(8,128)(2,1)} %emb_hbm.1, s32[1,256]{1,0:T(1,128)} %tgt_hbm.1), custom_call_target="tpu_custom_call" | custom-call | tf_op jit(solution)/shard_map/head/pallas_call | solution.py:253
  42.0 0.0 copy-start
  42.0 0.7 %copy-done = f32[1,768]{1,0:T(1,128)S(1)} copy-done((f32[1,768]{1,0:T(1,128)S(1)}, f32[1,768]{1,0:T(1,128)}, u32[]{:S(2)}) %copy-start) | copy-done | bytes 3096
  42.7 7.5 %exchange.1.box = f32[8,1,768]{2,1,0:T(1,128)S(1)} custom-call(f32[1,768]{1,0:T(1,128)S(1)} %copy-done), custom_call_target="tpu_custom_call" | custom-call | tf_op jit(solution)/shard_map/exchange/pallas_call | solution.py:279
  50.2 0.0 copy-done.1
  50.2 0.6 %finish.1 = (f32[1,256]{1,0:T(1,128)}, f32[1,256]{1,0:T(1,128)}, f32[1,128]{1,0:T(1,128)}, f32[1,256]{1,0:T(1,128)}) custom-call(f32[8,1,768]{2,1,0:T(1,128)S(1)} %exchange.1.box, s32[1,256]{1,0:T(1,128)S(1)} %copy-done.1), custom_call_target="tpu_custom_call" | custom-call | tf_op jit(solution)/shard_map/finish/pallas_call | solution.py:293
Async XLA Ops:
  0.6 49.6 %copy-start.1 = (s32[1,256]{1,0:T(1,128)S(1)}, s32[1,256]{1,0:T(1,128)}, u32[]{:S(2)}) copy-start(s32[1,256]{1,0:T(1,128)} %mask.1) | copy-start | bytes 3076
  42.0 0.7 %copy-start = (f32[1,768]{1,0:T(1,128)S(1)}, f32[1,768]{1,0:T(1,128)}, u32[]{:S(2)}) copy-start(f32[1,768]{1,0:T(1,128)} %head.1.stats_ref) | copy-start | bytes 9220

commit v3 on v2

v3 whole, which is shorter than its diff:
```python
import functools

import jax
import jax.numpy as jnp
from jax import lax
from jax.experimental import pallas as pl
from jax.experimental.pallas import tpu as pltpu
from jax.sharding import PartitionSpec as P

OPT_VOCAB = 50272
LN_EPS = 1e-5

TILE = 256
CHUNK = 256
PIECE = 64
LANES = 128
RING = 10
FIRST = 3
PARTS = 6
HID_PARTS = 4
NORM_ROWS = 32
HEAD_VMEM = 52 << 20
SMALL_VMEM = 1 << 20
F32 = jnp.float32


def head_kernel(hid_hbm, gain_hbm, bias_hbm, emb_hbm, tgt_hbm, stats_ref,
                h, ring, z, gain, bias, tgt, mean_b, rstd_b, part, m8, s8, t8, small_sem, hid_sem, ring_sem,
                first_sem, last_sem):
    tokens, width = h.shape
    rows = emb_hbm.shape[0]
    n_chunks = rows // CHUNK
    passes = width // (2 * TILE)
    part_width = width // PARTS
    part_passes = passes // PARTS
    hid_rows = tokens // HID_PARTS
    base = lax.axis_index("tp") * rows

    def hid_copy(i):
        at = pl.ds(i * hid_rows, hid_rows)
        return pltpu.make_async_copy(hid_hbm.at[0, at], h.at[at], hid_sem.at[i])

    def chunk_copy(c):
        slot = lax.rem(c, RING)
        return pltpu.make_async_copy(emb_hbm.at[pl.ds(c * CHUNK, CHUNK)], ring.at[slot], ring_sem.at[slot])

    def part_copy(c, i, sem):
        cols = pl.ds(i * part_width, part_width)
        return pltpu.make_async_copy(
            emb_hbm.at[pl.ds(c * CHUNK, CHUNK), cols], ring.at[lax.rem(c, RING), :, cols], sem)

    def first_copy(e, i):
        return part_copy(e, i, first_sem.at[e, i])

    def last_copy(e, i):
        return part_copy(n_chunks - 2 + e, i, last_sem.at[e, i])

    small = [pltpu.make_async_copy(src, dst, small_sem.at[i]) for i, (src, dst) in enumerate(
        ((gain_hbm, gain), (bias_hbm, bias), (tgt_hbm, tgt)))]

    for i in range(HID_PARTS):
        hid_copy(i).start()
    for copy in small:
        copy.start()
    for i in range(PARTS):
        for e in range(FIRST):
            first_copy(e, i).start(priority=1)
    for c in range(FIRST, RING):
        chunk_copy(c).start(priority=1)

    def lane_sum(r, n, fn):
        acc = [jnp.zeros((n, LANES), F32) for _ in range(2)]
        for c in range(width // LANES):
            acc[c % 2] += fn(h[pl.ds(r, n), pl.ds(c * LANES, LANES)].astype(F32))
        return acc[0] + acc[1]

    group = 16

    def mean_rows(i):
        for g in range(hid_rows // group):
            r = i * hid_rows + g * group
            part[pl.ds(r, group)] = lane_sum(r, group, lambda x: x)
        at = pl.ds(i * hid_rows, hid_rows)
        mean = jnp.sum(part[at], axis=-1, keepdims=True) * (1.0 / width)
        mean_b[at] = jnp.broadcast_to(mean, (hid_rows, LANES))

    def var_rows(i):
        for g in range(hid_rows // group):
            r = i * hid_rows + g * group
            mean = mean_b[pl.ds(r, group)]
            part[pl.ds(r, group)] = lane_sum(r, group, lambda x: (x - mean) * (x - mean))
        at = pl.ds(i * hid_rows, hid_rows)
        var = jnp.sum(part[at], axis=-1, keepdims=True) * (1.0 / width)
        rstd_b[at] = jnp.broadcast_to(lax.rsqrt(var + LN_EPS), (hid_rows, LANES))

    for i in range(HID_PARTS):
        hid_copy(i).wait()
        mean_rows(i)
        if i:
            var_rows(i - 1)
    var_rows(HID_PARTS - 1)

    for copy in small:
        copy.wait()
    m8[...] = jnp.full_like(m8, jnp.finfo(F32).min)
    s8[...] = jnp.zeros_like(s8)
    t8[...] = jnp.zeros_like(t8)

    def normalize(k, r=0, n=tokens):
        at, cols = pl.ds(r, n), pl.ds(k * TILE, TILE)
        wide = lambda x: jnp.concatenate([x] * (TILE // LANES), axis=1)
        x = h[at, cols].astype(F32)
        x = (x - wide(mean_b[at])) * wide(rstd_b[at]) * gain[:, cols] + bias[:, cols]
        h[at, cols] = x.astype(h.dtype)

    def matmuls(*accs):
        n_piece = CHUNK // PIECE
        accs = [[accs[(w * 2 + q) * n_piece:(w * 2 + q + 1) * n_piece] for q in range(2)] for w in range(4)]

        for which in accs:
            for q in which:
                for acc in q:
                    z[pl.ds(0, PIECE)] = pltpu.matmul_pop(acc)

        def push(j, q):
            cols = pl.ds((2 * j + q) * TILE, TILE)
            pltpu.matmul_push_rhs(h[:, cols], staging_register=j % 2, mxu_index=q, transpose=True)

        def accumulate(chunks, sets, j):
            def step(c, which, p, q):
                lhs = ring[lax.rem(c, RING), pl.ds(p * PIECE, PIECE), pl.ds((2 * j + q) * TILE, TILE)]
                pltpu.matmul_acc_lhs(
                    accs[which][q][p], lhs, load_staged_rhs=j % 2 if which == sets[0] and p == 0 else None)
            return [functools.partial(step, c, which, p, q)
                    for c, which in zip(chunks, sets) for p in range(n_piece) for q in range(2)]

        def drain(c, which, p):
            offset = base + c * CHUNK
            target = tgt[...] - offset
            limit = OPT_VOCAB - offset
            shape = (PIECE // 8, 8, tokens)
            logits = pltpu.matmul_pop(accs[which][0][p]) + pltpu.matmul_pop(accs[which][1][p])
            row = lax.broadcasted_iota(jnp.int32, logits.shape, 0) + p * PIECE
            logits = jnp.where(row < limit, logits, -jnp.inf)
            z[pl.ds(p * PIECE, PIECE)] = logits
            m8[1] = jnp.maximum(m8[1], jnp.max(logits.reshape(shape), axis=0))
            t8[...] += jnp.sum(jnp.where(row == target, logits, 0.0).reshape(shape), axis=0)

        def exps(p):
            top = m8[1]
            total = s8[...]
            if p == 0:
                total = total * jnp.exp(m8[0] - top)
                m8[0] = top
            e = jnp.exp(z[pl.ds(p * PIECE, PIECE)].reshape(PIECE // 8, 8, tokens) - top[None])
            s8[...] = total + jnp.sum(e, axis=0)

        def absorb(c, which):
            return [functools.partial(drain, c, which, p) for p in range(n_piece)] + [
                functools.partial(exps, p) for p in range(n_piece)]

        def sweep(chunks, sets, beside=(), wait=None, norm=False, last=False):
            beside = list(beside)
            per_pass = pl.cdiv(len(beside), passes - 3)
            for j in range(passes):
                if wait is not None and j % part_passes == 0:
                    wait(j // part_passes)
                def push_next():
                    for q in range(2):
                        if not (last and j + 1 == passes):
                            push((j + 1) % passes, q)

                steps = accumulate(chunks, sets, j)
                if norm and j + 1 < passes:
                    cut = len(steps) * 2 // 3
                    groups = [(2 * (j + 1) + q, r) for q in range(2) for r in range(0, tokens, NORM_ROWS)]
                    for i, step in enumerate(steps):
                        for k, r in groups[i * len(groups) // cut:(i + 1) * len(groups) // cut]:
                            normalize(k, r, NORM_ROWS)
                        if i == cut:
                            push_next()
                        step()
                else:
                    push_next()
                    for step in steps:
                        step()
                if j >= 2:
                    for step in beside[(j - 2) * per_pass:(j - 1) * per_pass]:
                        step()

        def first_wait(i):
            for e in range(FIRST):
                first_copy(e, i).wait()

        def last_wait(i):
            for e in range(2):
                last_copy(e, i).wait()

        for k in range(2):
            normalize(k)
        for q in range(2):
            push(0, q)
        sweep(range(FIRST), range(FIRST), wait=first_wait, norm=True)
        for step in absorb(0, 0):
            step()
        for c in range(RING, RING + FIRST - 2):
            chunk_copy(c).start(priority=1)

        def pair(c, sets, old, refill=True):
            for e in range(2):
                chunk_copy(c + e).wait()
            if refill:
                @pl.when(c + RING < n_chunks)
                def _():
                    for e in range(2):
                        chunk_copy(c - 2 + e + RING).start(priority=1)

                @pl.when(c + RING == n_chunks)
                def _():
                    for i in range(PARTS):
                        for e in range(2):
                            last_copy(e, i).start(priority=1)
            sweep((c, c + 1), sets, absorb(c - 2, old[0]) + absorb(c - 1, old[1]))

        def two_pairs(i, carry):
            c = FIRST + 4 * i
            pair(c, (3, 0), (1, 2))
            pair(c + 2, (1, 2), (3, 0))
            return carry

        lax.fori_loop(0, (n_chunks - FIRST) // 4, two_pairs, 0)
        c = n_chunks - 2
        sweep((c, c + 1), (3, 0), absorb(c - 2, 1) + absorb(c - 1, 2), wait=last_wait, last=True)
        for step in absorb(c, 3) + absorb(c + 1, 0):
            step()

    pl.run_scoped(matmuls, *[pltpu.ACC(q)((PIECE, TILE), F32)
                             for _ in range(4) for q in range(2) for _ in range(CHUNK // PIECE)])

    top = jnp.max(m8[0], axis=0, keepdims=True)
    total = jnp.sum(s8[...] * jnp.exp(m8[0] - top), axis=0, keepdims=True)
    picked = jnp.sum(t8[...], axis=0, keepdims=True)
    stats_ref[...] = jnp.concatenate([top, total, picked], axis=1)


def exchange_kernel(n_tp, stats_ref, out_ref, box, send_sem, recv_sem):
    me = lax.axis_index("tp")

    def peer(d):
        return lax.rem(me + d, n_tp)

    def exchange(d, slot):
        return pltpu.make_async_remote_copy(
            src_ref=stats_ref, dst_ref=box.at[slot], send_sem=send_sem.at[d], recv_sem=recv_sem.at[slot],
            device_id={"tp": peer(d)}, device_id_type=pl.DeviceIdType.MESH)

    barrier = pltpu.get_barrier_semaphore()
    for d in range(1, n_tp):
        pl.semaphore_signal(barrier, inc=1, device_id={"tp": peer(d)}, device_id_type=pl.DeviceIdType.MESH)
    pl.semaphore_wait(barrier, n_tp - 1)
    for d in range(1, n_tp):
        exchange(d, me).start()
    box[me] = stats_ref[...]
    for d in range(1, n_tp):
        exchange(d, peer(d)).wait_recv()
    out_ref[...] = box[...]
    for d in range(1, n_tp):
        exchange(d, me).wait_send()


def finish_kernel(box, mask, norm_ref, logp_ref, seq_ref, top_ref):
    n_tp, _, width = box.shape
    tokens = width // 3
    boxes = [box[i] for i in range(n_tp)]
    top = functools.reduce(jnp.maximum, [x[:, :tokens] for x in boxes])
    total = sum(x[:, tokens:2 * tokens] * jnp.exp(x[:, :tokens] - top) for x in boxes)
    picked = sum(x[:, 2 * tokens:] for x in boxes)
    log_norm = top + jnp.log(total)
    token_logp = (picked - log_norm) * mask[...].astype(F32)
    norm_ref[...] = log_norm
    logp_ref[...] = token_logp
    top_ref[...] = top - log_norm
    seq_ref[...] = jnp.broadcast_to(jnp.sum(token_logp, axis=-1, keepdims=True), seq_ref.shape)


def solution(mesh):
    n_tp = mesh.shape["tp"]

    def local_part(hidden, ln_gain, ln_bias, embedding, targets, score_mask):
        prompts, tokens, width = hidden.shape
        rows = embedding.shape[0]
        n_chunks = rows // CHUNK
        assert prompts == 1 and tokens == TILE and rows % CHUNK == 0 and width % (2 * TILE * PARTS) == 0
        assert (n_chunks - FIRST) % 4 == 2 and n_chunks > RING + FIRST + 2
        row = jax.ShapeDtypeStruct((prompts, tokens), F32)
        stats = pl.pallas_call(
            head_kernel,
            out_shape=jax.ShapeDtypeStruct((1, 3 * tokens), F32),
            in_specs=[pl.BlockSpec(memory_space=pl.ANY)] * 5,
            out_specs=pl.BlockSpec(memory_space=pltpu.VMEM),
            scratch_shapes=[
                pltpu.VMEM((tokens, width), hidden.dtype),
                pltpu.VMEM((RING, CHUNK, width), embedding.dtype),
                pltpu.VMEM((CHUNK, tokens), F32),
                pltpu.VMEM((1, width), F32),
                pltpu.VMEM((1, width), F32),
                pltpu.VMEM((1, tokens), jnp.int32),
                pltpu.VMEM((tokens, LANES), F32),
                pltpu.VMEM((tokens, LANES), F32),
                pltpu.VMEM((tokens, LANES), F32),
                pltpu.VMEM((2, 8, tokens), F32),
                pltpu.VMEM((8, tokens), F32),
                pltpu.VMEM((8, tokens), F32),
                pltpu.SemaphoreType.DMA((3,)),
                pltpu.SemaphoreType.DMA((HID_PARTS,)),
                pltpu.SemaphoreType.DMA((RING,)),
                pltpu.SemaphoreType.DMA((FIRST, PARTS)),
                pltpu.SemaphoreType.DMA((2, PARTS)),
            ],
            compiler_params=pltpu.CompilerParams(vmem_limit_bytes=HEAD_VMEM),
            name="head",
        )(*[pltpu.with_memory_space_constraint(x, pltpu.HBM) for x in (
            hidden, ln_gain.reshape(1, width), ln_bias.reshape(1, width), embedding, targets)])
        vmem = pl.BlockSpec(memory_space=pltpu.VMEM)
        boxes = pl.pallas_call(
            functools.partial(exchange_kernel, n_tp),
            out_shape=jax.ShapeDtypeStruct((n_tp, 1, 3 * tokens), F32),
            in_specs=[vmem],
            out_specs=vmem,
            scratch_shapes=[
                pltpu.VMEM((n_tp, 1, 3 * tokens), F32),
                pltpu.SemaphoreType.DMA((n_tp,)),
                pltpu.SemaphoreType.DMA((n_tp,)),
            ],
            compiler_params=pltpu.CompilerParams(
                collective_id=0, has_side_effects=True, vmem_limit_bytes=SMALL_VMEM),
            name="exchange",
        )(stats)
        log_norm, token_logp, seq, top_logp = pl.pallas_call(
            finish_kernel,
            out_shape=(row, row, jax.ShapeDtypeStruct((prompts, LANES), F32), row),
            in_specs=[vmem] * 2,
            out_specs=[vmem] * 4,
            compiler_params=pltpu.CompilerParams(vmem_limit_bytes=SMALL_VMEM),
            name="finish",
        )(boxes, score_mask)
        return log_norm, token_logp, seq[:, 0], top_logp

    row_spec = P("dp", None)
    return jax.shard_map(local_part, mesh=mesh,
                         in_specs=(P("dp", None, None), P(), P(), P("tp", None), row_spec, row_spec),
                         out_specs=(row_spec, row_spec, P("dp"), row_spec), check_vma=False)
```

time: 50.9 us -> 48.3 us (0.949)
  Pallas kernels: 49.5 us -> 47.6 us
  local copies, waits for them, and re-layouts: 0.67 us -> 0.01 us
    pallas_call x1, Pallas kernels: 41.4 us -> 39.4 us  [local_part(): pl.pallas_call(head_kernel, out_shape=jax.ShapeDtypeStruct((1, 3 * tokens...]
    unnamed x4 -> x2, local copies, waits for them, and re-layouts: 0.67 us -> 0.01 us
where the time goes in v3:
time: 48.3 us
  Pallas kernels  47.6 us (99%)
  between operations  0.66 us (1%)
    pallas_call x1, Pallas kernels, local_part(): pl.pallas_call(head_kernel, out_shape=jax.ShapeDtypeStruct((1, 3 * tokens...  39.4 us
    pallas_call x1, Pallas kernels, local_part(): pl.pallas_call(functools.partial(exchange_kernel, n_tp), out_shape=jax.Sh...  7.6 us

profile of v3, /device:TPU:113, one launch (start us, length us, event | category | flops | bytes accessed | tf_op | source)
XLA Modules:
  0.0 48.3 jit_solution(7763248563705758519)
XLA Ops:
  0.6 0.0 copy-start
  0.6 39.4 %head.1.stats_ref = f32[1,768]{1,0:T(1,128)S(1)} custom-call(bf16[1,256,9216]{2,1,0:T(8,128)(2,1)} %hid_hbm.1, f32[1,9216]{1,0:T(1,128)} %bitcast.4, f32[1,9216]{1,0:T(1,128)} %bitcast.5, bf16[6400,9216]{1,0:T(8,128)(2,1)} %emb_hbm.1, s32[1,256]{1,0:T(1,128)} %tgt_hbm.1), custom_call_target="tpu_custom_call" | custom-call | tf_op jit(solution)/shard_map/head/pallas_call | solution.py:296
  40.0 7.6 %exchange.1.box = f32[8,1,768]{2,1,0:T(1,128)S(1)} custom-call(f32[1,768]{1,0:T(1,128)S(1)} %head.1.stats_ref), custom_call_target="tpu_custom_call" | custom-call | tf_op jit(solution)/shard_map/exchange/pallas_call | solution.py:325
  47.6 0.0 copy-done
  47.6 0.6 %finish.1 = (f32[1,256]{1,0:T(1,128)}, f32[1,256]{1,0:T(1,128)}, f32[1,128]{1,0:T(1,128)}, f32[1,256]{1,0:T(1,128)}) custom-call(f32[8,1,768]{2,1,0:T(1,128)S(1)} %exchange.1.box, s32[1,256]{1,0:T(1,128)S(1)} %copy-done), custom_call_target="tpu_custom_call" | custom-call | tf_op jit(solution)/shard_map/finish/pallas_call | solution.py:339
Async XLA Ops:
  0.6 47.0 %copy-start = (s32[1,256]{1,0:T(1,128)S(1)}, s32[1,256]{1,0:T(1,128)}, u32[]{:S(2)}) copy-start(s32[1,256]{1,0:T(1,128)} %mask.1) | copy-start | bytes 3076

commit v4 on v3

--- a/solution.py
+++ b/solution.py
@@ -14,7 +14,7 @@
 CHUNK = 256
 PIECE = 64
 LANES = 128
-RING = 10
+RING = 8
 FIRST = 3
 PARTS = 6
 HID_PARTS = 4
@@ -62,11 +62,7 @@
         hid_copy(i).start()
     for copy in small:
         copy.start()
-    for i in range(PARTS):
-        for e in range(FIRST):
-            first_copy(e, i).start(priority=1)
-    for c in range(FIRST, RING):
-        chunk_copy(c).start(priority=1)
+    early = list(range(FIRST, RING))
 
     def lane_sum(r, n, fn):
         acc = [jnp.zeros((n, LANES), F32) for _ in range(2)]
@@ -95,9 +91,14 @@
 
     for i in range(HID_PARTS):
         hid_copy(i).wait()
+        if i == 0:
+            for k in range(PARTS):
+                for e in range(FIRST):
+                    first_copy(e, k).start(priority=1)
         mean_rows(i)
         if i:
             var_rows(i - 1)
+    chunk_copy(early.pop(0)).start(priority=1)
     var_rows(HID_PARTS - 1)
 
     for copy in small:
@@ -191,6 +192,8 @@
         def first_wait(i):
             for e in range(FIRST):
                 first_copy(e, i).wait()
+            for _ in range(len(early) - (PARTS - 1 - i) * len(early) // (PARTS - i)):
+                chunk_copy(early.pop(0)).start(priority=1)
 
         def last_wait(i):
             for e in range(2):

time: 48.3 us -> 48.4 us (level)
  no operation moved by 1% of the time
where the time goes in v4:
time: 48.4 us; the launch traced here: 48.3 us
  Pallas kernels  47.6 us (98%)
  between operations  0.66 us (1%)
    pallas_call x1, Pallas kernels, local_part(): pl.pallas_call(head_kernel, out_shape=jax.ShapeDtypeStruct((1, 3 * tokens...  39.4 us
    pallas_call x1, Pallas kernels, local_part(): pl.pallas_call(functools.partial(exchange_kernel, n_tp), out_shape=jax.Sh...  7.6 us

profile of v4, /device:TPU:113, one launch (start us, length us, event | category | flops | bytes accessed | tf_op | source)
XLA Modules:
  0.0 48.3 jit_solution(16029627245408544724)
XLA Ops:
  0.6 0.0 copy-start
  0.6 39.4 %head.1.stats_ref = f32[1,768]{1,0:T(1,128)S(1)} custom-call(bf16[1,256,9216]{2,1,0:T(8,128)(2,1)} %hid_hbm.1, f32[1,9216]{1,0:T(1,128)} %bitcast.4, f32[1,9216]{1,0:T(1,128)} %bitcast.5, bf16[6400,9216]{1,0:T(8,128)(2,1)} %emb_hbm.1, s32[1,256]{1,0:T(1,128)} %tgt_hbm.1), custom_call_target="tpu_custom_call" | custom-call | tf_op jit(solution)/shard_map/head/pallas_call | solution.py:299
  40.0 7.6 %exchange.1.box = f32[8,1,768]{2,1,0:T(1,128)S(1)} custom-call(f32[1,768]{1,0:T(1,128)S(1)} %head.1.stats_ref), custom_call_target="tpu_custom_call" | custom-call | tf_op jit(solution)/shard_map/exchange/pallas_call | solution.py:328
  47.6 0.0 copy-done
  47.6 0.6 %finish.1 = (f32[1,256]{1,0:T(1,128)}, f32[1,256]{1,0:T(1,128)}, f32[1,128]{1,0:T(1,128)}, f32[1,256]{1,0:T(1,128)}) custom-call(f32[8,1,768]{2,1,0:T(1,128)S(1)} %exchange.1.box, s32[1,256]{1,0:T(1,128)S(1)} %copy-done), custom_call_target="tpu_custom_call" | custom-call | tf_op jit(solution)/shard_map/finish/pallas_call | solution.py:342
Async XLA Ops:
  0.6 47.0 %copy-start = (s32[1,256]{1,0:T(1,128)S(1)}, s32[1,256]{1,0:T(1,128)}, u32[]{:S(2)}) copy-start(s32[1,256]{1,0:T(1,128)} %mask.1) | copy-start | bytes 3076

commit v5 on v4

--- a/solution.py
+++ b/solution.py
@@ -160,12 +160,12 @@
             return [functools.partial(drain, c, which, p) for p in range(n_piece)] + [
                 functools.partial(exps, p) for p in range(n_piece)]
 
-        def sweep(chunks, sets, beside=(), wait=None, norm=False, last=False):
+        def sweep(chunks, sets, beside=(), hooks=None, norm=False, last=False):
             beside = list(beside)
             per_pass = pl.cdiv(len(beside), passes - 3)
             for j in range(passes):
-                if wait is not None and j % part_passes == 0:
-                    wait(j // part_passes)
+                if hooks and j in hooks:
+                    hooks[j]()
                 def push_next():
                     for q in range(2):
                         if not (last and j + 1 == passes):
@@ -199,41 +199,61 @@
             for e in range(2):
                 last_copy(e, i).wait()
 
+        def part_hooks(wait):
+            return {part_passes * i - 1: functools.partial(wait, i) for i in range(1, PARTS)}
+
+        def chunk_wait(c):
+            for e in range(2):
+                chunk_copy(c + e).wait()
+
         for k in range(2):
             normalize(k)
         for q in range(2):
             push(0, q)
-        sweep(range(FIRST), range(FIRST), wait=first_wait, norm=True)
+        first_wait(0)
+        sweep(range(FIRST), range(FIRST), norm=True,
+              hooks={**part_hooks(first_wait), passes - 1: functools.partial(chunk_wait, FIRST)})
         for step in absorb(0, 0):
             step()
         for c in range(RING, RING + FIRST - 2):
             chunk_copy(c).start(priority=1)
 
-        def pair(c, sets, old, refill=True):
+        def pair(c, sets, old, refill=None, ahead=chunk_wait):
+            def turn():
+                if refill is not None:
+                    refill(c - 2 + RING)
+                ahead(c + 2)
+
+            sweep((c, c + 1), sets, absorb(c - 2, old[0]) + absorb(c - 1, old[1]), hooks={passes - 2: turn})
+
+        def refill(c):
             for e in range(2):
-                chunk_copy(c + e).wait()
-            if refill:
-                @pl.when(c + RING < n_chunks)
-                def _():
+                chunk_copy(c + e).start(priority=1)
+
+        def refill_or_last(c):
+            @pl.when(c < n_chunks - 2)
+            def _():
+                refill(c)
+
+            @pl.when(c == n_chunks - 2)
+            def _():
+                for i in range(PARTS):
                     for e in range(2):
-                        chunk_copy(c - 2 + e + RING).start(priority=1)
-
-                @pl.when(c + RING == n_chunks)
-                def _():
-                    for i in range(PARTS):
-                        for e in range(2):
-                            last_copy(e, i).start(priority=1)
-            sweep((c, c + 1), sets, absorb(c - 2, old[0]) + absorb(c - 1, old[1]))
+                        last_copy(e, i).start(priority=1)
 
         def two_pairs(i, carry):
             c = FIRST + 4 * i
-            pair(c, (3, 0), (1, 2))
-            pair(c + 2, (1, 2), (3, 0))
+            pair(c, (3, 0), (1, 2), refill)
+            pair(c + 2, (1, 2), (3, 0), refill_or_last)
             return carry
 
-        lax.fori_loop(0, (n_chunks - FIRST) // 4, two_pairs, 0)
+        trips = (n_chunks - FIRST) // 4 - 1
+        lax.fori_loop(0, trips, two_pairs, 0)
+        c = FIRST + 4 * trips
+        pair(c, (3, 0), (1, 2))
+        pair(c + 2, (1, 2), (3, 0), ahead=lambda _: last_wait(0))
         c = n_chunks - 2
-        sweep((c, c + 1), (3, 0), absorb(c - 2, 1) + absorb(c - 1, 2), wait=last_wait, last=True)
+        sweep((c, c + 1), (3, 0), absorb(c - 2, 1) + absorb(c - 1, 2), hooks=part_hooks(last_wait), last=True)
         for step in absorb(c, 3) + absorb(c + 1, 0):
             step()
 
@@ -294,7 +314,7 @@
         rows = embedding.shape[0]
         n_chunks = rows // CHUNK
         assert prompts == 1 and tokens == TILE and rows % CHUNK == 0 and width % (2 * TILE * PARTS) == 0
-        assert (n_chunks - FIRST) % 4 == 2 and n_chunks > RING + FIRST + 2
+        assert (n_chunks - FIRST) % 4 == 2 and n_chunks == RING + FIRST + 4 * ((n_chunks - FIRST) // 4 - 1) - 2
         row = jax.ShapeDtypeStruct((prompts, tokens), F32)
         stats = pl.pallas_call(
             head_kernel,

time: 48.4 us -> 48.7 us (level)
  no operation moved by 1% of the time
where the time goes in v5:
time: 48.7 us; the launch traced here: 48.6 us
  Pallas kernels  47.9 us (98%)
  between operations  0.66 us (1%)
    pallas_call x1, Pallas kernels, local_part(): pl.pallas_call(head_kernel, out_shape=jax.ShapeDtypeStruct((1, 3 * tokens...  39.7 us
    pallas_call x1, Pallas kernels, local_part(): pl.pallas_call(functools.partial(exchange_kernel, n_tp), out_shape=jax.Sh...  7.58 us

profile of v5, /device:TPU:113, one launch (start us, length us, event | category | flops | bytes accessed | tf_op | source)
XLA Modules:
  0.0 48.6 jit_solution(10955140394395404088)
XLA Ops:
  0.6 0.0 copy-start
  0.6 39.7 %head.1.stats_ref = f32[1,768]{1,0:T(1,128)S(1)} custom-call(bf16[1,256,9216]{2,1,0:T(8,128)(2,1)} %hid_hbm.1, f32[1,9216]{1,0:T(1,128)} %bitcast.4, f32[1,9216]{1,0:T(1,128)} %bitcast.5, bf16[6400,9216]{1,0:T(8,128)(2,1)} %emb_hbm.1, s32[1,256]{1,0:T(1,128)} %tgt_hbm.1), custom_call_target="tpu_custom_call" | custom-call | tf_op jit(solution)/shard_map/head/pallas_call | solution.py:319
  40.4 7.6 %exchange.1.box = f32[8,1,768]{2,1,0:T(1,128)S(1)} custom-call(f32[1,768]{1,0:T(1,128)S(1)} %head.1.stats_ref), custom_call_target="tpu_custom_call" | custom-call | tf_op jit(solution)/shard_map/exchange/pallas_call | solution.py:348
  48.0 0.0 copy-done
  48.0 0.6 %finish.1 = (f32[1,256]{1,0:T(1,128)}, f32[1,256]{1,0:T(1,128)}, f32[1,128]{1,0:T(1,128)}, f32[1,256]{1,0:T(1,128)}) custom-call(f32[8,1,768]{2,1,0:T(1,128)S(1)} %exchange.1.box, s32[1,256]{1,0:T(1,128)S(1)} %copy-done), custom_call_target="tpu_custom_call" | custom-call | tf_op jit(solution)/shard_map/finish/pallas_call | solution.py:362
Async XLA Ops:
  0.6 47.3 %copy-start = (s32[1,256]{1,0:T(1,128)S(1)}, s32[1,256]{1,0:T(1,128)}, u32[]{:S(2)}) copy-start(s32[1,256]{1,0:T(1,128)} %mask.1) | copy-start | bytes 3076

commit v6 on v4

--- a/solution.py
+++ b/solution.py
@@ -40,14 +40,19 @@
         at = pl.ds(i * hid_rows, hid_rows)
         return pltpu.make_async_copy(hid_hbm.at[0, at], h.at[at], hid_sem.at[i])
 
-    def chunk_copy(c):
-        slot = lax.rem(c, RING)
-        return pltpu.make_async_copy(emb_hbm.at[pl.ds(c * CHUNK, CHUNK)], ring.at[slot], ring_sem.at[slot])
+    def slot(c):
+        return lax.rem(c + 1, RING)
+
+    def pair_copy(c):
+        at = pl.ds(pl.multiple_of(c * CHUNK, CHUNK), 2 * CHUNK)
+        to = pl.ds(pl.multiple_of(slot(c) * CHUNK, CHUNK), 2 * CHUNK)
+        return pltpu.make_async_copy(emb_hbm.at[at], ring.at[to], ring_sem.at[slot(c)])
 
     def part_copy(c, i, sem):
+        at = pl.ds(pl.multiple_of(c * CHUNK, CHUNK), CHUNK)
+        to = pl.ds(pl.multiple_of(slot(c) * CHUNK, CHUNK), CHUNK)
         cols = pl.ds(i * part_width, part_width)
-        return pltpu.make_async_copy(
-            emb_hbm.at[pl.ds(c * CHUNK, CHUNK), cols], ring.at[lax.rem(c, RING), :, cols], sem)
+        return pltpu.make_async_copy(emb_hbm.at[at, cols], ring.at[to, cols], sem)
 
     def first_copy(e, i):
         return part_copy(e, i, first_sem.at[e, i])
@@ -62,7 +67,7 @@
         hid_copy(i).start()
     for copy in small:
         copy.start()
-    early = list(range(FIRST, RING))
+    early = list(range(FIRST, RING - 2, 2))
 
     def lane_sum(r, n, fn):
         acc = [jnp.zeros((n, LANES), F32) for _ in range(2)]
@@ -98,7 +103,7 @@
         mean_rows(i)
         if i:
             var_rows(i - 1)
-    chunk_copy(early.pop(0)).start(priority=1)
+    pair_copy(early.pop(0)).start(priority=1)
     var_rows(HID_PARTS - 1)
 
     for copy in small:
@@ -129,7 +134,8 @@
 
         def accumulate(chunks, sets, j):
             def step(c, which, p, q):
-                lhs = ring[lax.rem(c, RING), pl.ds(p * PIECE, PIECE), pl.ds((2 * j + q) * TILE, TILE)]
+                at = pl.ds(pl.multiple_of(slot(c) * CHUNK + p * PIECE, PIECE), PIECE)
+                lhs = ring[at, pl.ds((2 * j + q) * TILE, TILE)]
                 pltpu.matmul_acc_lhs(
                     accs[which][q][p], lhs, load_staged_rhs=j % 2 if which == sets[0] and p == 0 else None)
             return [functools.partial(step, c, which, p, q)
@@ -192,12 +198,8 @@
         def first_wait(i):
             for e in range(FIRST):
                 first_copy(e, i).wait()
-            for _ in range(len(early) - (PARTS - 1 - i) * len(early) // (PARTS - i)):
-                chunk_copy(early.pop(0)).start(priority=1)
-
-        def last_wait(i):
-            for e in range(2):
-                last_copy(e, i).wait()
+            if i % 3 == 1 and early:
+                pair_copy(early.pop(0)).start(priority=1)
 
         for k in range(2):
             normalize(k)
@@ -206,23 +208,21 @@
         sweep(range(FIRST), range(FIRST), wait=first_wait, norm=True)
         for step in absorb(0, 0):
             step()
-        for c in range(RING, RING + FIRST - 2):
-            chunk_copy(c).start(priority=1)
-
-        def pair(c, sets, old, refill=True):
-            for e in range(2):
-                chunk_copy(c + e).wait()
-            if refill:
-                @pl.when(c + RING < n_chunks)
-                def _():
-                    for e in range(2):
-                        chunk_copy(c - 2 + e + RING).start(priority=1)
-
-                @pl.when(c + RING == n_chunks)
-                def _():
+        pair_copy(FIRST - 4 + RING).start(priority=1)
+        def refill(c):
+            @pl.when(c < n_chunks - 2)
+            def _():
+                pair_copy(c).start(priority=1)
+
+            @pl.when(c == n_chunks - 2)
+            def _():
+                for e in range(2):
                     for i in range(PARTS):
-                        for e in range(2):
-                            last_copy(e, i).start(priority=1)
+                        last_copy(e, i).start(priority=1)
+
+        def pair(c, sets, old):
+            pair_copy(c).wait()
+            refill(c - 2 + RING)
             sweep((c, c + 1), sets, absorb(c - 2, old[0]) + absorb(c - 1, old[1]))
 
         def two_pairs(i, carry):
@@ -231,10 +231,11 @@
             pair(c + 2, (1, 2), (3, 0))
             return carry
 
-        lax.fori_loop(0, (n_chunks - FIRST) // 4, two_pairs, 0)
+        lax.fori_loop(0, (n_chunks - FIRST - 2) // 4, two_pairs, 0)
         c = n_chunks - 2
-        sweep((c, c + 1), (3, 0), absorb(c - 2, 1) + absorb(c - 1, 2), wait=last_wait, last=True)
-        for step in absorb(c, 3) + absorb(c + 1, 0):
+        sweep((c,), (3,), absorb(c - 2, 1) + absorb(c - 1, 2), wait=lambda i: last_copy(0, i).wait())
+        sweep((c + 1,), (0,), absorb(c, 3), wait=lambda i: last_copy(1, i).wait(), last=True)
+        for step in absorb(c + 1, 0):
             step()
 
     pl.run_scoped(matmuls, *[pltpu.ACC(q)((PIECE, TILE), F32)
@@ -294,7 +295,7 @@
         rows = embedding.shape[0]
         n_chunks = rows // CHUNK
         assert prompts == 1 and tokens == TILE and rows % CHUNK == 0 and width % (2 * TILE * PARTS) == 0
-        assert (n_chunks - FIRST) % 4 == 2 and n_chunks > RING + FIRST + 2
+        assert (n_chunks - FIRST) % 4 == 2 and n_chunks > RING + FIRST and RING % 2 == 0
         row = jax.ShapeDtypeStruct((prompts, tokens), F32)
         stats = pl.pallas_call(
             head_kernel,
@@ -303,7 +304,7 @@
             out_specs=pl.BlockSpec(memory_space=pltpu.VMEM),
             scratch_shapes=[
                 pltpu.VMEM((tokens, width), hidden.dtype),
-                pltpu.VMEM((RING, CHUNK, width), embedding.dtype),
+                pltpu.VMEM((RING * CHUNK, width), embedding.dtype),
                 pltpu.VMEM((CHUNK, tokens), F32),
                 pltpu.VMEM((1, width), F32),
                 pltpu.VMEM((1, width), F32),

time: 48.4 us -> 48.6 us (level)
  no operation moved by 1% of the time
where the time goes in v6:
time: 48.6 us; the launch traced here: 48.5 us
  Pallas kernels  47.9 us (99%)
  between operations  0.66 us (1%)
    pallas_call x1, Pallas kernels, local_part(): pl.pallas_call(head_kernel, out_shape=jax.ShapeDtypeStruct((1, 3 * tokens...  39.6 us
    pallas_call x1, Pallas kernels, local_part(): pl.pallas_call(functools.partial(exchange_kernel, n_tp), out_shape=jax.Sh...  7.59 us

profile of v6, /device:TPU:113, one launch (start us, length us, event | category | flops | bytes accessed | tf_op | source)
XLA Modules:
  0.0 48.5 jit_solution(17307778847556114055)
XLA Ops:
  0.6 0.0 copy-start
  0.6 39.6 %head.1.stats_ref = f32[1,768]{1,0:T(1,128)S(1)} custom-call(bf16[1,256,9216]{2,1,0:T(8,128)(2,1)} %hid_hbm.1, f32[1,9216]{1,0:T(1,128)} %bitcast.4, f32[1,9216]{1,0:T(1,128)} %bitcast.5, bf16[6400,9216]{1,0:T(8,128)(2,1)} %emb_hbm.1, s32[1,256]{1,0:T(1,128)} %tgt_hbm.1), custom_call_target="tpu_custom_call" | custom-call | tf_op jit(solution)/shard_map/head/pallas_call | solution.py:300
  40.3 7.6 %exchange.1.box = f32[8,1,768]{2,1,0:T(1,128)S(1)} custom-call(f32[1,768]{1,0:T(1,128)S(1)} %head.1.stats_ref), custom_call_target="tpu_custom_call" | custom-call | tf_op jit(solution)/shard_map/exchange/pallas_call | solution.py:329
  47.9 0.0 copy-done
  47.9 0.6 %finish.1 = (f32[1,256]{1,0:T(1,128)}, f32[1,256]{1,0:T(1,128)}, f32[1,128]{1,0:T(1,128)}, f32[1,256]{1,0:T(1,128)}) custom-call(f32[8,1,768]{2,1,0:T(1,128)S(1)} %exchange.1.box, s32[1,256]{1,0:T(1,128)S(1)} %copy-done), custom_call_target="tpu_custom_call" | custom-call | tf_op jit(solution)/shard_map/finish/pallas_call | solution.py:343
Async XLA Ops:
  0.6 47.3 %copy-start = (s32[1,256]{1,0:T(1,128)S(1)}, s32[1,256]{1,0:T(1,128)}, u32[]{:S(2)}) copy-start(s32[1,256]{1,0:T(1,128)} %mask.1) | copy-start | bytes 3076
